TPU v7x, 32 devices: a whole 2x2x4 slice. The times are simulated.
32 devices in a mesh: face: 8 (over z, core), sub: 4 (over y, x).
Axes of the slice: x: 2, y: 2, z: 4, core: 2. Of those that a mesh axis runs over, the one named last changes fastest.
Arguments:
- mesh_latent: bfloat16 [8192, 512], P(('face', 'sub')), may hold values from -6 to 6
- edge_latent: bfloat16 [65536, 512], P(('face', 'sub')), may hold values from -6 to 6
- grid_features: bfloat16 [8192, 384], P(('face', 'sub')), may hold values from -6 to 6
- senders: int32 [65536], P(('face', 'sub')), may hold values from 0 to 383, as said below
- receivers: int32 [65536], P(('face', 'sub')), may hold values from 0 to 255
- send_lists: int32 [32, 4, 32], P(('face', 'sub')), may hold values from -1 to 255, as said below
- link_sources: int32 [16384], P(('face', 'sub')), may hold values from 0 to 255
- link_targets: int32 [16384], P(('face', 'sub')), may hold values from 0 to 255
- node_area: float32 [8192], P(('face', 'sub')), may hold values from 0.25 to 4.5
- grid_weight: bfloat16 [384, 512], P(None, 'sub'), may hold values from -0.3125 to 0.3125
- encode_weight: bfloat16 [1024, 512], P('sub'), may hold values from -0.1875 to 0.1875
- edge_first: bfloat16 [1, 1536, 512], P(None, 'sub'), may hold values from -0.15625 to 0.15625
- edge_second: bfloat16 [1, 512, 512], P(None, 'sub'), may hold values from -0.25 to 0.25
- node_first: bfloat16 [1, 1024, 512], P(None, 'sub'), may hold values from -0.1875 to 0.1875
- node_second: bfloat16 [1, 512, 512], P(None, 'sub'), may hold values from -0.25 to 0.25
Outputs:
- mesh_result: bfloat16 [8192, 512], P(('face', 'sub'))
- edge_result: bfloat16 [65536, 512], P(('face', 'sub'))
- masses: float32 [1, 512], replicated
Inputs may be any that keep to these rules, and one draw needn't show every extreme that they name: `send_lists`: entries are the sending partition's own node numbers, or -1 for an unused slot; in every list the used slots come first, hold distinct nodes and number 32 // 2 or more; for every list number some partition uses all 32 slots. `senders`: A value below 256 names one of the partition's own nodes; 256 + d * 32 + k names slot k of the list with number d that the partition receives, and that slot is always a used one.
All inputs are finite; a program needn't handle non-finite values.
Results may differ from a plain program's by a relative error of at most 0.008.
Values may be sent and summed in bfloat16 or wider, within the bound.
A program may use at most 64 MiB of HBM per device.

v0:
```python
import functools

import jax
import jax.numpy as jnp
from jax import lax
from jax.experimental import pallas as pl
from jax.experimental.pallas import tpu as pltpu
from jax.sharding import PartitionSpec as P

MESH = pl.DeviceIdType.MESH
CHUNK = 512
QUARTERED = (1, 2)
BF = jnp.bfloat16
F32 = jnp.float32


def silu(v):
    return v / (1.0 + jnp.exp(-v))


def mm(a, b):
    return jnp.dot(a, b, preferred_element_type=F32)


def mm_t(a, b):
    return lax.dot_general(a, b, (((0,), (0,)), ((), ())), preferred_element_type=F32)


def hot(rows, index):
    ids = lax.broadcasted_iota(jnp.int32, (rows, index.shape[1]), 0)
    return jnp.where(ids == index, 1.0, 0.0).astype(BF)


def kernel(
    n_face, n_sub,
    mesh_hbm, edge_hbm, grid_hbm, send_hbm, recv_hbm, lists_hbm, src_hbm, dst_hbm, area_hbm,
    wg, we, w1, w2, v1, v2,
    lat_out, edge_hbm_out, mass_out,
    gg, ge, g1, g2, h1, h2,
    mesh_ref, grid_ref, send_ref, recv_ref, lists_ref, src_ref, dst_ref, area_ref,
    edges, picks, back, table, proj, halo, sums_a, sums_b, total,
    s1, r1, s2, r2, s3, r3, hs, hr, as_, ar, bs, br, ein, eout, win, pin,
):
    face, sub = lax.axis_index("face"), lax.axis_index("sub")
    core = lax.rem(face, 2)
    partner = face + 1 - 2 * core
    level = lax.rem(face // 2, 2)
    beside = face + 2 - 4 * level
    nodes, width = mesh_ref.shape
    chunks = edges.shape[0] // CHUNK

    def load_edges(i):
        rows = pl.ds(pl.multiple_of(i * CHUNK, CHUNK), CHUNK)
        return pltpu.make_async_copy(edge_hbm.at[rows], edges.at[rows], ein.at[i])

    def store_edges(i):
        rows = pl.ds(pl.multiple_of(i * CHUNK, CHUNK), CHUNK)
        return pltpu.make_async_copy(edges.at[rows], edge_hbm_out.at[rows], eout.at[i])

    shards = [wg, we, w1.at[0], w2.at[0], v1.at[0], v2.at[0]]
    wholes = [gg, ge, g1, g2, h1, h2]

    def own(w):
        rows = shards[w].shape[0]
        slot = gg.at[sub] if w == 0 else wholes[w].at[pl.ds(pl.multiple_of(sub * rows, rows), rows)]
        return pltpu.make_async_copy(shards[w], slot, win.at[w])

    pairs = [(send_hbm, send_ref), (recv_hbm, recv_ref), (src_hbm, src_ref), (dst_hbm, dst_ref),
             (grid_hbm, grid_ref), (mesh_hbm, mesh_ref), (lists_hbm, lists_ref), (area_hbm, area_ref)]
    loads = [pltpu.make_async_copy(a, b, pin.at[i]) for i, (a, b) in enumerate(pairs)]
    for w in range(6):
        own(w).start()
    for copy in loads:
        copy.start()
    for i in range(chunks):
        load_edges(i).start()

    barrier = pltpu.get_barrier_semaphore()
    for k in range(1, n_sub):
        pl.semaphore_signal(barrier, inc=1, device_id=(face, lax.rem(sub + k, n_sub)), device_id_type=MESH)
    for k in range(1, n_face):
        pl.semaphore_signal(barrier, inc=1, device_id=(lax.rem(face + k, n_face), sub), device_id_type=MESH)
    pl.semaphore_wait(barrier, n_sub + n_face - 2)

    def half_of(w, owner):
        rows = shards[w].shape[0]
        half = rows // 2
        if w == 0:
            return gg.at[owner, pl.ds(pl.multiple_of(core * half, half), half)]
        return wholes[w].at[pl.ds(pl.multiple_of(owner * rows + core * half, half), half)]

    def quarter_of(w, owner):
        rows = shards[w].shape[0]
        piece = rows // 4
        start = (core * 2 + level) * piece
        if w == 0:
            return gg.at[owner, pl.ds(pl.multiple_of(start, piece), piece)]
        return wholes[w].at[pl.ds(pl.multiple_of(owner * rows + start, piece), piece)]

    def outward(w, k):
        part = quarter_of(w, sub) if w in QUARTERED else half_of(w, sub)
        return pltpu.make_async_remote_copy(
            src_ref=part, dst_ref=part,
            send_sem=s1.at[w, k], recv_sem=r1.at[w, k],
            device_id=(face, lax.rem(sub + k, n_sub)), device_id_type=MESH)

    def upward(w, k):
        part = quarter_of(w, lax.rem(sub + n_sub - k, n_sub))
        return pltpu.make_async_remote_copy(
            src_ref=part, dst_ref=part, send_sem=s3.at[w, k], recv_sem=r3.at[w, k],
            device_id=(beside, sub), device_id_type=MESH)

    def across(w, k):
        part = half_of(w, lax.rem(sub + n_sub - k, n_sub))
        return pltpu.make_async_remote_copy(
            src_ref=part, dst_ref=part, send_sem=s2.at[w, k], recv_sem=r2.at[w, k],
            device_id=(partner, sub), device_id_type=MESH)

    def send(w):
        own(w).wait()
        for k in range(1, n_sub):
            outward(w, k).start()

    for w in range(4):
        send(w)
    for copy in loads:
        copy.wait()

    def climb(w):
        for k in range(1, n_sub):
            if w in QUARTERED:
                outward(w, k).wait_recv()
                upward(w, k).start()

    def pass_on(w):
        for k in range(1, n_sub):
            if w in QUARTERED:
                upward(w, k).wait_recv()
            else:
                outward(w, k).wait_recv()
            across(w, k).start()

    def arrive(w):
        for k in range(1, n_sub):
            across(w, k).wait_recv()

    slots = nodes + 4 * halo.shape[1]

    def mark(i, carry):
        cols = pl.ds(pl.multiple_of(i * CHUNK, CHUNK), CHUNK)
        here = hot(nodes, recv_ref[:, cols])
        back[:, cols] = here
        both = jnp.concatenate([hot(slots, send_ref[:, cols]), here], axis=0)
        picks[cols, :] = both.T
        return carry

    lax.fori_loop(0, chunks, mark, 0)
    to_node = hot(nodes, dst_ref[...])
    link_pick = jnp.concatenate([hot(grid_ref.shape[0], src_ref[...]), to_node], axis=0)

    pass_on(0)
    climb(1)
    arrive(0)
    grid = jnp.concatenate([mm(grid_ref[...], gg[j]) for j in range(n_sub)], axis=1)
    grid = silu(grid).astype(BF)
    pass_on(1)
    climb(2)
    arrive(1)
    rows = grid_ref.shape[0]
    from_grid = mm(grid, ge[:width, :]).astype(BF)
    from_mesh = mm(mesh_ref[...], ge[width:, :]).astype(BF)
    message = silu(mm_t(link_pick, jnp.concatenate([from_grid, from_mesh], axis=0))).astype(BF)
    latent = (mesh_ref[...].astype(F32) + mm(to_node, message)).astype(BF)
    table[...] = latent

    size = halo.shape[1]
    for d in range(4):
        halo[d] = mm_t(hot(nodes, lists_ref[0, d:d + 1, :]), latent).astype(BF)

    def border(d):
        step = (1, n_face - 1, 1, n_sub - 1)[d]
        to = (lax.rem(face + step, n_face), sub) if d < 2 else (face, lax.rem(sub + step, n_sub))
        return pltpu.make_async_remote_copy(
            src_ref=halo.at[d], dst_ref=halo.at[4 + d], send_sem=hs.at[d], recv_sem=hr.at[d],
            device_id=to, device_id_type=MESH)

    for d in range(4):
        border(d).start()
    send(4)
    send(5)

    pass_on(2)
    arrive(2)
    proj[:nodes, :] = mm(latent, g1[width:2 * width, :]).astype(BF)
    proj[slots:, :] = mm(latent, g1[2 * width:, :]).astype(BF)
    for d in range(4):
        border(d).wait_recv()
    outer = jnp.concatenate([halo[4 + d] for d in range(4)], axis=0)
    proj[nodes:slots, :] = mm(outer, g1[width:2 * width, :]).astype(BF)
    pass_on(3)
    arrive(3)

    total[...] = jnp.zeros_like(total)
    for i in range(chunks):
        load_edges(i).wait()

    def update(i, carry):
        cols = pl.ds(pl.multiple_of(i * CHUNK, CHUNK), CHUNK)
        edge = edges[cols, :]
        before = mm(edge, g1[:width, :]) + mm(picks[cols, :], proj[...])
        hidden = silu(before).astype(BF)
        new = (edge.astype(F32) + mm(hidden, g2[...])).astype(BF)
        edges[cols, :] = new
        total[...] += mm(back[:, cols], new)
        return carry

    lax.fori_loop(0, chunks // 2, update, 0)
    climb(4)
    lax.fori_loop(chunks // 2, chunks, update, 0)
    pass_on(4)
    pass_on(5)
    for i in range(chunks):
        store_edges(i).start()
    arrive(4)
    incoming = total[...].astype(BF)
    hidden = silu(mm(table[...], h1[:width, :]) + mm(incoming, h1[width:, :])).astype(BF)
    arrive(5)
    final = (table[...].astype(F32) + mm(hidden, h2[...])).astype(BF)
    lat_out[...] = final
    part = jnp.dot(area_ref[...], final.astype(F32), precision=lax.Precision.HIGHEST, preferred_element_type=F32)

    def share_sub(k):
        return pltpu.make_async_remote_copy(
            src_ref=sums_a.at[sub], dst_ref=sums_a.at[sub], send_sem=as_.at[k], recv_sem=ar.at[k],
            device_id=(face, lax.rem(sub + k, n_sub)), device_id_type=MESH)

    def share_face(k):
        return pltpu.make_async_remote_copy(
            src_ref=sums_b.at[face], dst_ref=sums_b.at[face], send_sem=bs.at[k], recv_sem=br.at[k],
            device_id=(lax.rem(face + k, n_face), sub), device_id_type=MESH)

    sums_a[sub] = part
    for k in range(1, n_sub):
        share_sub(k).start()
    for k in range(1, n_sub):
        share_sub(k).wait_recv()
    sums_b[face] = jnp.sum(sums_a[...], axis=0)
    for k in range(1, n_face):
        share_face(k).start()
    for k in range(1, n_face):
        share_face(k).wait_recv()
    mass_out[...] = jnp.sum(sums_b[...], axis=0) / (nodes * n_face * n_sub)

    for w in range(6):
        for k in range(1, n_sub):
            outward(w, k).wait_send()
            across(w, k).wait_send()
            if w in QUARTERED:
                upward(w, k).wait_send()
    for d in range(4):
        border(d).wait_send()
    for k in range(1, n_sub):
        share_sub(k).wait_send()
    for k in range(1, n_face):
        share_face(k).wait_send()
    for i in range(chunks):
        store_edges(i).wait()


def per_device(
    mesh_latent, edge_latent, grid_features, senders, receivers, send_lists, link_sources,
    link_targets, node_area, grid_weight, encode_weight, edge_first, edge_second, node_first,
    node_second,
):
    n_face, n_sub = lax.axis_size("face"), lax.axis_size("sub")
    nodes, width = mesh_latent.shape
    count = edge_latent.shape[0]
    size = send_lists.shape[2]
    slots = nodes + 4 * size
    chunks = count // CHUNK
    dma = pltpu.SemaphoreType.DMA
    vmem = pl.BlockSpec(memory_space=pltpu.VMEM)
    hbm = pl.BlockSpec(memory_space=pl.ANY)
    whole = [pltpu.VMEM((n_sub * w.shape[-2], width), BF)
             for w in (encode_weight, edge_first, edge_second, node_first, node_second)]
    return pl.pallas_call(
        functools.partial(kernel, n_face, n_sub),
        out_shape=(
            jax.ShapeDtypeStruct(mesh_latent.shape, BF),
            jax.ShapeDtypeStruct(edge_latent.shape, BF),
            jax.ShapeDtypeStruct((1, width), F32),
        ),
        in_specs=[hbm] * 15,
        out_specs=(vmem, hbm, vmem),
        scratch_shapes=[
            pltpu.VMEM((n_sub,) + grid_weight.shape, BF), *whole,
            pltpu.VMEM(mesh_latent.shape, BF), pltpu.VMEM(grid_features.shape, BF),
            pltpu.VMEM((1, count), jnp.int32), pltpu.VMEM((1, count), jnp.int32),
            pltpu.VMEM(send_lists.shape, jnp.int32),
            pltpu.VMEM((1, link_sources.shape[0]), jnp.int32),
            pltpu.VMEM((1, link_targets.shape[0]), jnp.int32),
            pltpu.VMEM((1, nodes), F32),
            pltpu.VMEM(edge_latent.shape, BF),
            pltpu.VMEM((count, slots + nodes), BF),
            pltpu.VMEM((nodes, count), BF),
            pltpu.VMEM((nodes, width), BF),
            pltpu.VMEM((slots + nodes, width), BF),
            pltpu.VMEM((8, size, width), BF),
            pltpu.VMEM((n_sub, 1, width), F32),
            pltpu.VMEM((n_face, 1, width), F32),
            pltpu.VMEM((nodes, width), F32),
            *[dma((6, n_sub))] * 6,
            dma((4,)), dma((4,)), dma((n_sub,)), dma((n_sub,)), dma((n_face,)), dma((n_face,)),
            dma((chunks,)), dma((chunks,)), dma((6,)), dma((8,)),
        ],
        compiler_params=pltpu.CompilerParams(
            collective_id=0, has_side_effects=True, vmem_limit_bytes=67043328
        ),
    )(
        mesh_latent, edge_latent, grid_features, senders.reshape(1, -1), receivers.reshape(1, -1),
        send_lists, link_sources.reshape(1, -1), link_targets.reshape(1, -1),
        node_area.reshape(1, -1), grid_weight, encode_weight, edge_first, edge_second, node_first,
        node_second,
    )


def solution(mesh):
    both = P(("face", "sub"))
    in_specs = (both,) * 9 + (P(None, "sub"), P("sub", None)) + (P(None, "sub", None),) * 4
    return jax.shard_map(
        per_device, mesh=mesh, in_specs=in_specs, out_specs=(both, both, P()), check_vma=False
    )
```

profile of v0, /device:TPU:0, one launch (start us, length us, event | category | flops | bytes accessed | tf_op | source)
XLA Modules:
  0.0 50.7 jit_solution(7028937128890408916)
XLA Ops:
  0.6 44.7 %shard_map.166 = (bf16[256,512]{1,0:T(8,128)(2,1)}, bf16[2048,512]{1,0:T(8,128)(2,1)}, f32[1,512]{1,0:T(1,128)}) custom-call(bf16[256,512]{1,0:T(8,128)(2,1)} %mesh_hbm.1, bf16[2048,512]{1,0:T(8,128)(2,1)} %edge_hbm.1, bf16[256,384]{1,0:T(8,128)(2,1)} %grid_hbm.1, s32[1,2048]{1,0:T(1,128)} %bitcast.5, s32[1,2048]{1,0:T(1,128)} %bitcast.6, ...), custom_call_target="tpu_custom_call" | custom-call | tf_op jit(solution)/shard_map/pallas_call | solution.py:286
  45.4 1.7 %copy.21 = bf16[256,512]{1,0:T(8,128)(2,1)} copy(bf16[256,512]{1,0:T(8,128)(2,1)} %get-tuple-element.6) | data formatting | bytes 524288
  47.1 0.0 copy-start
  47.1 3.0 %copy.22 = bf16[2048,512]{1,0:T(8,128)(2,1)} copy(bf16[2048,512]{1,0:T(8,128)(2,1)} %get-tuple-element.7) | data formatting | bytes 4194304
  50.1 0.0 copy-done
  50.1 0.6 %copy.23 = f32[1,512]{1,0:T(1,128)} copy(f32[1,512]{1,0:T(1,128)S(1)} %copy-done) | data formatting | bytes 4096
Async XLA Ops:
  47.1 3.0 %copy-start = (f32[1,512]{1,0:T(1,128)S(1)}, f32[1,512]{1,0:T(1,128)}, u32[]{:S(2)}) copy-start(f32[1,512]{1,0:T(1,128)} %get-tuple-element.8) | copy-start | bytes 6148
where the time goes:
time: 50.9 us; the launch traced here: 50.7 us
  Pallas kernels  44.7 us (88%)
  local copies, waits for them, and re-layouts  5.3 us (10%)
  between operations  0.65 us (1%)
    pallas_call x1, Pallas kernels, per_device(): pl.pallas_call(functools.partial(kernel, n_face, n_sub), out_shape=(jax.S...  44.7 us
    unnamed x5, local copies, waits for them, and re-layouts  5.3 us

commit v1 on v0

--- a/solution.py
+++ b/solution.py
@@ -9,6 +9,7 @@
 
 MESH = pl.DeviceIdType.MESH
 CHUNK = 512
+LANES = 128
 QUARTERED = (1, 2)
 BF = jnp.bfloat16
 F32 = jnp.float32
@@ -35,11 +36,11 @@
     n_face, n_sub,
     mesh_hbm, edge_hbm, grid_hbm, send_hbm, recv_hbm, lists_hbm, src_hbm, dst_hbm, area_hbm,
     wg, we, w1, w2, v1, v2,
-    lat_out, edge_hbm_out, mass_out,
+    lat_out, edges, mass_out,
     gg, ge, g1, g2, h1, h2,
     mesh_ref, grid_ref, send_ref, recv_ref, lists_ref, src_ref, dst_ref, area_ref,
-    edges, picks, back, table, proj, halo, sums_a, sums_b, total,
-    s1, r1, s2, r2, s3, r3, hs, hr, as_, ar, bs, br, ein, eout, win, pin,
+    picks, back, table, proj, halo, parts, total, hiddens, area_col,
+    s1, r1, s2, r2, s3, r3, hs, hr, ms, mr, ein, win, pin,
 ):
     face, sub = lax.axis_index("face"), lax.axis_index("sub")
     core = lax.rem(face, 2)
@@ -52,10 +53,6 @@
     def load_edges(i):
         rows = pl.ds(pl.multiple_of(i * CHUNK, CHUNK), CHUNK)
         return pltpu.make_async_copy(edge_hbm.at[rows], edges.at[rows], ein.at[i])
-
-    def store_edges(i):
-        rows = pl.ds(pl.multiple_of(i * CHUNK, CHUNK), CHUNK)
-        return pltpu.make_async_copy(edges.at[rows], edge_hbm_out.at[rows], eout.at[i])
 
     shards = [wg, we, w1.at[0], w2.at[0], v1.at[0], v2.at[0]]
     wholes = [gg, ge, g1, g2, h1, h2]
@@ -75,12 +72,12 @@
     for i in range(chunks):
         load_edges(i).start()
 
+    others = [(lax.rem(face + a, n_face), lax.rem(sub + b, n_sub))
+              for a in range(n_face) for b in range(n_sub) if a or b]
     barrier = pltpu.get_barrier_semaphore()
-    for k in range(1, n_sub):
-        pl.semaphore_signal(barrier, inc=1, device_id=(face, lax.rem(sub + k, n_sub)), device_id_type=MESH)
-    for k in range(1, n_face):
-        pl.semaphore_signal(barrier, inc=1, device_id=(lax.rem(face + k, n_face), sub), device_id_type=MESH)
-    pl.semaphore_wait(barrier, n_sub + n_face - 2)
+    for peer in others:
+        pl.semaphore_signal(barrier, inc=1, device_id=peer, device_id_type=MESH)
+    pl.semaphore_wait(barrier, len(others))
 
     def half_of(w, owner):
         rows = shards[w].shape[0]
@@ -155,6 +152,17 @@
         return carry
 
     lax.fori_loop(0, chunks, mark, 0)
+    for i in range(chunks):
+        load_edges(i).wait()
+    total[...] = jnp.zeros_like(total)
+
+    def collect(i, carry):
+        cols = pl.ds(pl.multiple_of(i * CHUNK, CHUNK), CHUNK)
+        total[...] += mm(back[:, cols], edges[cols, :])
+        return carry
+
+    lax.fori_loop(0, chunks, collect, 0)
+    area_col[...] = jnp.broadcast_to(area_ref[...], (LANES, nodes)).T
     to_node = hot(nodes, dst_ref[...])
     link_pick = jnp.concatenate([hot(grid_ref.shape[0], src_ref[...]), to_node], axis=0)
 
@@ -200,56 +208,49 @@
     pass_on(3)
     arrive(3)
 
-    total[...] = jnp.zeros_like(total)
-    for i in range(chunks):
-        load_edges(i).wait()
-
-    def update(i, carry):
+    into = jnp.zeros((nodes, width), F32)
+
+    def first(i, into):
         cols = pl.ds(pl.multiple_of(i * CHUNK, CHUNK), CHUNK)
-        edge = edges[cols, :]
-        before = mm(edge, g1[:width, :]) + mm(picks[cols, :], proj[...])
+        before = mm(edges[cols, :], g1[:width, :]) + mm(picks[cols, :], proj[...])
         hidden = silu(before).astype(BF)
-        new = (edge.astype(F32) + mm(hidden, g2[...])).astype(BF)
-        edges[cols, :] = new
-        total[...] += mm(back[:, cols], new)
-        return carry
-
-    lax.fori_loop(0, chunks // 2, update, 0)
+        hiddens[cols, :] = hidden
+        return into + mm(back[:, cols], hidden)
+
+    into = lax.fori_loop(0, chunks // 2, first, into)
     climb(4)
-    lax.fori_loop(chunks // 2, chunks, update, 0)
+    into = lax.fori_loop(chunks // 2, chunks, first, into)
     pass_on(4)
     pass_on(5)
-    for i in range(chunks):
-        store_edges(i).start()
+    high = into.astype(BF)
+    low = (into - high.astype(F32)).astype(BF)
+    incoming = (total[...] + (mm(high, g2[...]) + mm(low, g2[...]))).astype(BF)
     arrive(4)
-    incoming = total[...].astype(BF)
     hidden = silu(mm(table[...], h1[:width, :]) + mm(incoming, h1[width:, :])).astype(BF)
     arrive(5)
     final = (table[...].astype(F32) + mm(hidden, h2[...])).astype(BF)
     lat_out[...] = final
-    part = jnp.dot(area_ref[...], final.astype(F32), precision=lax.Precision.HIGHEST, preferred_element_type=F32)
-
-    def share_sub(k):
-        return pltpu.make_async_remote_copy(
-            src_ref=sums_a.at[sub], dst_ref=sums_a.at[sub], send_sem=as_.at[k], recv_sem=ar.at[k],
-            device_id=(face, lax.rem(sub + k, n_sub)), device_id_type=MESH)
-
-    def share_face(k):
-        return pltpu.make_async_remote_copy(
-            src_ref=sums_b.at[face], dst_ref=sums_b.at[face], send_sem=bs.at[k], recv_sem=br.at[k],
-            device_id=(lax.rem(face + k, n_face), sub), device_id_type=MESH)
-
-    sums_a[sub] = part
-    for k in range(1, n_sub):
-        share_sub(k).start()
-    for k in range(1, n_sub):
-        share_sub(k).wait_recv()
-    sums_b[face] = jnp.sum(sums_a[...], axis=0)
-    for k in range(1, n_face):
-        share_face(k).start()
-    for k in range(1, n_face):
-        share_face(k).wait_recv()
-    mass_out[...] = jnp.sum(sums_b[...], axis=0) / (nodes * n_face * n_sub)
+    weight = jnp.concatenate([area_col[...]] * (width // LANES), axis=1)
+    me = face * n_sub + sub
+    parts[me] = jnp.sum(final.astype(F32) * weight, axis=0, keepdims=True)
+
+    def share(k):
+        return pltpu.make_async_remote_copy(
+            src_ref=parts.at[me], dst_ref=parts.at[me], send_sem=ms.at[k], recv_sem=mr.at[k],
+            device_id=others[k], device_id_type=MESH)
+
+    for k in range(len(others)):
+        share(k).start()
+
+    def second(i, carry):
+        cols = pl.ds(pl.multiple_of(i * CHUNK, CHUNK), CHUNK)
+        edges[cols, :] = (edges[cols, :].astype(F32) + mm(hiddens[cols, :], g2[...])).astype(BF)
+        return carry
+
+    lax.fori_loop(0, chunks, second, 0)
+    for k in range(len(others)):
+        share(k).wait_recv()
+    mass_out[...] = jnp.sum(parts[...], axis=0) / (nodes * n_face * n_sub)
 
     for w in range(6):
         for k in range(1, n_sub):
@@ -259,12 +260,17 @@
                 upward(w, k).wait_send()
     for d in range(4):
         border(d).wait_send()
-    for k in range(1, n_sub):
-        share_sub(k).wait_send()
-    for k in range(1, n_face):
-        share_face(k).wait_send()
-    for i in range(chunks):
-        store_edges(i).wait()
+    for k in range(len(others)):
+        share(k).wait_send()
+
+
+def put(lat, edges, mass, lat_out, edges_out, mass_out, sems):
+    pairs = [(edges, edges_out), (lat, lat_out), (mass, mass_out)]
+    copies = [pltpu.make_async_copy(a, b, sems.at[i]) for i, (a, b) in enumerate(pairs)]
+    for copy in copies:
+        copy.start()
+    for copy in copies:
+        copy.wait()
 
 
 def per_device(
@@ -280,18 +286,19 @@
     chunks = count // CHUNK
     dma = pltpu.SemaphoreType.DMA
     vmem = pl.BlockSpec(memory_space=pltpu.VMEM)
-    hbm = pl.BlockSpec(memory_space=pl.ANY)
+    hbm = pl.BlockSpec(memory_space=pltpu.HBM)
+    anywhere = pl.BlockSpec(memory_space=pl.ANY)
     whole = [pltpu.VMEM((n_sub * w.shape[-2], width), BF)
              for w in (encode_weight, edge_first, edge_second, node_first, node_second)]
-    return pl.pallas_call(
+    results = pl.pallas_call(
         functools.partial(kernel, n_face, n_sub),
         out_shape=(
-            jax.ShapeDtypeStruct(mesh_latent.shape, BF),
-            jax.ShapeDtypeStruct(edge_latent.shape, BF),
-            jax.ShapeDtypeStruct((1, width), F32),
+            pltpu.VMEM(mesh_latent.shape, BF),
+            pltpu.VMEM(edge_latent.shape, BF),
+            pltpu.VMEM((1, width), F32),
         ),
         in_specs=[hbm] * 15,
-        out_specs=(vmem, hbm, vmem),
+        out_specs=(vmem, vmem, vmem),
         scratch_shapes=[
             pltpu.VMEM((n_sub,) + grid_weight.shape, BF), *whole,
             pltpu.VMEM(mesh_latent.shape, BF), pltpu.VMEM(grid_features.shape, BF),
@@ -300,21 +307,21 @@
             pltpu.VMEM((1, link_sources.shape[0]), jnp.int32),
             pltpu.VMEM((1, link_targets.shape[0]), jnp.int32),
             pltpu.VMEM((1, nodes), F32),
-            pltpu.VMEM(edge_latent.shape, BF),
             pltpu.VMEM((count, slots + nodes), BF),
             pltpu.VMEM((nodes, count), BF),
             pltpu.VMEM((nodes, width), BF),
             pltpu.VMEM((slots + nodes, width), BF),
             pltpu.VMEM((8, size, width), BF),
-            pltpu.VMEM((n_sub, 1, width), F32),
-            pltpu.VMEM((n_face, 1, width), F32),
+            pltpu.VMEM((n_face * n_sub, 1, width), F32),
             pltpu.VMEM((nodes, width), F32),
+            pltpu.VMEM(edge_latent.shape, BF),
+            pltpu.VMEM((nodes, LANES), F32),
             *[dma((6, n_sub))] * 6,
-            dma((4,)), dma((4,)), dma((n_sub,)), dma((n_sub,)), dma((n_face,)), dma((n_face,)),
-            dma((chunks,)), dma((chunks,)), dma((6,)), dma((8,)),
+            dma((4,)), dma((4,)), dma((n_face * n_sub,)), dma((n_face * n_sub,)),
+            dma((chunks,)), dma((6,)), dma((8,)),
         ],
         compiler_params=pltpu.CompilerParams(
-            collective_id=0, has_side_effects=True, vmem_limit_bytes=67043328
+            collective_id=0, has_side_effects=True, vmem_limit_bytes=62000000
         ),
     )(
         mesh_latent, edge_latent, grid_features, senders.reshape(1, -1), receivers.reshape(1, -1),
@@ -322,6 +329,14 @@
         node_area.reshape(1, -1), grid_weight, encode_weight, edge_first, edge_second, node_first,
         node_second,
     )
+    return pl.pallas_call(
+        put,
+        out_shape=tuple(jax.ShapeDtypeStruct(r.shape, r.dtype) for r in results),
+        in_specs=[anywhere] * 3,
+        out_specs=(anywhere,) * 3,
+        scratch_shapes=[dma((3,))],
+        compiler_params=pltpu.CompilerParams(vmem_limit_bytes=1 << 20),
+    )(*results)
 
 
 def solution(mesh):

time: 50.9 us -> 44.4 us (0.87)
  local copies, waits for them, and re-layouts: 5.3 us -> 0 us
  Pallas kernels: 44.7 us -> 43.7 us
    unnamed x5 -> x0, local copies, waits for them, and re-layouts: 5.3 us -> none
    pallas_call x1 -> x2, Pallas kernels: 44.7 us -> 43.7 us  [the longest x1 42.2 us: per_device(): pl.pallas_call(functools.partial(kernel, n_face, n_sub), out_shape=(pltpu...]
where the time goes in v1:
time: 44.4 us; the launch traced here: 44.3 us
  Pallas kernels  43.7 us (98%)
  between operations  0.64 us (1%)
    pallas_call x1, Pallas kernels, per_device(): pl.pallas_call(functools.partial(kernel, n_face, n_sub), out_shape=(pltpu...  42.2 us
    pallas_call x1, Pallas kernels, per_device(): pl.pallas_call(put, out_shape=tuple((jax.ShapeDtypeStruct(r.shape, r.dtyp...  1.42 us

profile of v1, /device:TPU:0, one launch (start us, length us, event | category | flops | bytes accessed | tf_op | source)
XLA Modules:
  0.0 44.3 jit_solution(4682263433623925607)
XLA Ops:
  0.6 42.2 %shard_map.166 = (bf16[256,512]{1,0:T(8,128)(2,1)S(1)}, bf16[2048,512]{1,0:T(8,128)(2,1)S(1)}, f32[1,512]{1,0:T(1,128)S(1)}) custom-call(bf16[256,512]{1,0:T(8,128)(2,1)} %mesh_hbm.1, bf16[2048,512]{1,0:T(8,128)(2,1)} %edge_hbm.1, bf16[256,384]{1,0:T(8,128)(2,1)} %grid_hbm.1, s32[1,2048]{1,0:T(1,128)} %bitcast.5, s32[1,2048]{1,0:T(1,128)} %bitcast.6, ...), custom_call_target="tpu_custom_call" | custom-call | tf_op jit(solution)/shard_map/pallas_call | solution.py:293
  42.9 1.4 %shard_map.167 = (bf16[256,512]{1,0:T(8,128)(2,1)}, bf16[2048,512]{1,0:T(8,128)(2,1)}, f32[1,512]{1,0:T(1,128)}) custom-call(bf16[256,512]{1,0:T(8,128)(2,1)S(1)} %get-tuple-element.6.lat, bf16[2048,512]{1,0:T(8,128)(2,1)S(1)} %get-tuple-element.7.edges, f32[1,512]{1,0:T(1,128)S(1)} %get-tuple-element.8.mass), custom_call_target="tpu_custom_call" | custom-call | tf_op jit(solution)/shard_map/pallas_call | solution.py:332

commit v2 on v1

v2 whole, which is shorter than its diff:
```python
import functools

import jax
import jax.numpy as jnp
from jax import lax
from jax.experimental import pallas as pl
from jax.experimental.pallas import tpu as pltpu
from jax.sharding import PartitionSpec as P

MESH = pl.DeviceIdType.MESH
CHUNK = 512
LANES = 128
LEVELLED = (1, 4)
BF = jnp.bfloat16
F32 = jnp.float32


def silu(v):
    return v / (1.0 + jnp.exp(-v))


def mm(a, b):
    return jnp.dot(a, b, preferred_element_type=F32)


def mm_t(a, b):
    return lax.dot_general(a, b, (((0,), (0,)), ((), ())), preferred_element_type=F32)


def hot(rows, index):
    ids = lax.broadcasted_iota(jnp.int32, (rows, index.shape[1]), 0)
    return jnp.where(ids == index, 1.0, 0.0).astype(BF)


PLAN = (
    ("first", 1), ("first", 0), ("second", 0), ("second", 1), ("first", 4), ("turn", 1), ("turn", 0),
    ("first", 2), ("direct", 1), ("last", 1), ("turn", 4), ("last", 0), ("second", 2), ("links", None),
    ("direct", 0), ("lift1", 1), ("mark", None), ("turn", 2), ("collect", None), ("lift2", 1), ("first", 5),
    ("lift3", 1), ("second", 4), ("first", 3), ("last", 4), ("arrive", 0), ("embed", None), ("second", 3),
    ("lift1", 4), ("arrive", 1), ("encode", None), ("ring", None), ("second", 5), ("direct", 2), ("last", 2),
    ("direct", 4), ("turn", 5), ("arrive", 2), ("turn", 3), ("project", None), ("direct", 3), ("hide0", None),
    ("direct", 5), ("lift2", 4), ("last", 5), ("last", 3), ("lift3", 4), ("hide1", None), ("arrive", 3),
    ("gather", None),
)


def kernel(
    n_face, n_sub,
    mesh_hbm, edge_hbm, grid_hbm, send_hbm, recv_hbm, lists_hbm, src_hbm, dst_hbm, area_hbm,
    wg, we, w1, w2, v1, v2,
    lat_out, edges, mass_out,
    gg, ge, g1, g2, h1, h2,
    mesh_ref, grid_ref, send_ref, recv_ref, lists_ref, src_ref, dst_ref, area_ref,
    picks, back, link_pick, table, proj, halo, parts, total, into, hiddens, area_col,
    s1, r1, s2, r2, s3, r3, hs, hr, ms, mr, ein, win, pin,
):
    face, sub = lax.axis_index("face"), lax.axis_index("sub")
    core = lax.rem(face, 2)
    partner = face + 1 - 2 * core
    level = lax.rem(face // 2, 2)
    beside = face + 2 - 4 * level
    nodes, width = mesh_ref.shape
    chunks = edges.shape[0] // CHUNK
    size = halo.shape[1]
    slots = nodes + 4 * size

    load_edges = pltpu.make_async_copy(edge_hbm, edges, ein)

    shards = [wg, we, w1.at[0], w2.at[0], v1.at[0], v2.at[0]]
    wholes = [gg, ge, g1, g2, h1, h2]

    def rows_of(w, owner, start, count):
        rows = shards[w].shape[0]
        return wholes[w].at[pl.ds(pl.multiple_of(owner * rows + start, count), count)]

    def own(w):
        return pltpu.make_async_copy(shards[w], rows_of(w, sub, 0, shards[w].shape[0]), win.at[w])

    pairs = [(send_hbm, send_ref), (recv_hbm, recv_ref), (src_hbm, src_ref), (dst_hbm, dst_ref),
             (grid_hbm, grid_ref), (mesh_hbm, mesh_ref), (lists_hbm, lists_ref), (area_hbm, area_ref)]
    loads = [pltpu.make_async_copy(a, b, pin.at[i]) for i, (a, b) in enumerate(pairs)]
    for w in range(6):
        own(w).start()
    for copy in loads:
        copy.start()
    load_edges.start()

    others = [(lax.rem(face + a, n_face), lax.rem(sub + b, n_sub))
              for a in range(n_face) for b in range(n_sub) if a or b]
    barrier = pltpu.get_barrier_semaphore()
    for peer in others:
        pl.semaphore_signal(barrier, inc=1, device_id=peer, device_id_type=MESH)
    pl.semaphore_wait(barrier, len(others))

    bits = [1 << b for b in range(n_sub.bit_length() - 1)]
    orders = (bits, bits[::-1])
    masks = range(1, n_sub)

    def across_bits(mask):
        index = sub
        for bit in bits:
            if mask & bit:
                index = index + bit - 2 * bit * lax.rem(index // bit, 2)
        return index

    def top(path, mask):
        return max(t for t, bit in enumerate(orders[path]) if mask & bit)

    def piece(w, path, mask, other_level=False):
        rows = shards[w].shape[0]
        if w in LEVELLED:
            count = rows // 8
            at = 1 - level if other_level else level
            start = (core * 4 + at * 2 + path) * count
        else:
            count = rows // 4
            start = (core * 2 + path) * count
        return rows_of(w, across_bits(mask), start, count)

    final = len(bits) - 1
    groups = [[(p, m) for m in masks for p in (0, 1) if top(p, m) == t] for t in range(final)]
    groups.append([(p, m) for p in (0, 1) for m in bits if top(p, m) == final])
    groups.append([(p, m) for m in masks for p in (0, 1) if top(p, m) == final and m not in bits])
    turns, direct, last = range(final), (final,), (final + 1,)
    group_of = {pm: g for g, group in enumerate(groups) for pm in group}

    def settle(w, count, sem):
        rows = wholes[w].at[pl.ds(0, count)]
        pltpu.make_async_copy(rows, rows, sem).wait()

    def cut(w):
        return shards[w].shape[0] // (8 if w in LEVELLED else 4)

    def outward(w, path, mask):
        bit = orders[path][top(path, mask)]
        part = piece(w, path, mask - bit)
        return pltpu.make_async_remote_copy(
            src_ref=part, dst_ref=part, send_sem=s1.at[w], recv_sem=r1.at[w, group_of[path, mask]],
            device_id=(face, across_bits(bit)), device_id_type=MESH)

    def upward(w, path, mask):
        part = piece(w, path, mask)
        at = LEVELLED.index(w)
        return pltpu.make_async_remote_copy(
            src_ref=part, dst_ref=part, send_sem=s3.at[at], recv_sem=r3.at[at, group_of[path, mask]],
            device_id=(beside, sub), device_id_type=MESH)

    def across(w, path, mask, lifted):
        part = piece(w, path, mask, lifted)
        return pltpu.make_async_remote_copy(
            src_ref=part, dst_ref=part, send_sem=s2.at[w], recv_sem=r2.at[w],
            device_id=(partner, sub), device_id_type=MESH)

    def begin(w):
        own(w).wait()
        for p in (0, 1):
            outward(w, p, orders[p][0]).start()

    def rest(w):
        for p in (0, 1):
            for bit in orders[p][1:]:
                outward(w, p, bit).start()

    def take(which, w):
        for g in which:
            if not groups[g]:
                continue
            settle(w, len(groups[g]) * cut(w), r1.at[w, g])
            for p, m in groups[g]:
                for bit in orders[p][top(p, m) + 1:]:
                    outward(w, p, m + bit).start()
                if w in LEVELLED:
                    upward(w, p, m).start()
                across(w, p, m, False).start()

    def lift(which, w):
        for g in which:
            if not groups[g]:
                continue
            settle(w, len(groups[g]) * cut(w), r3.at[LEVELLED.index(w), g])
            for p, m in groups[g]:
                across(w, p, m, True).start()

    def arrive(w):
        settle(w, (n_sub - 1) * shards[w].shape[0] // 2, r2.at[w])

    def border(d):
        step = (1, n_face - 1, 1, n_sub - 1)[d]
        to = (lax.rem(face + step, n_face), sub) if d < 2 else (face, lax.rem(sub + step, n_sub))
        return pltpu.make_async_remote_copy(
            src_ref=halo.at[d], dst_ref=halo.at[4 + d], send_sem=hs, recv_sem=hr,
            device_id=to, device_id_type=MESH)

    def ready():
        while loads:
            loads.pop().wait()

    def mark():
        ready()

        def step(i, carry):
            cols = pl.ds(pl.multiple_of(i * CHUNK, CHUNK), CHUNK)
            here = hot(nodes, recv_ref[:, cols])
            back[:, cols] = here
            both = jnp.concatenate([hot(slots, send_ref[:, cols]), here], axis=0)
            picks[cols, :] = both.T
            return carry

        lax.fori_loop(0, chunks, step, 0)

    def collect():
        load_edges.wait()
        total[...] = mm(back[...], edges[...])
        into[...] = jnp.zeros_like(into)
        area_col[...] = jnp.broadcast_to(area_ref[...], (LANES, nodes)).T

    grids = grid_ref.shape[0]

    def links():
        ready()
        link_pick[:grids, :] = hot(grids, src_ref[...])
        link_pick[grids:, :] = hot(nodes, dst_ref[...])

    def embed():
        depth = grid_ref.shape[1]
        grid = jnp.concatenate([mm(grid_ref[...], gg[j * depth:(j + 1) * depth, :]) for j in range(n_sub)], axis=1)
        table[...] = silu(grid).astype(BF)

    def encode():
        from_grid = mm(table[...], ge[:width, :]).astype(BF)
        from_mesh = mm(mesh_ref[...], ge[width:, :]).astype(BF)
        both = jnp.concatenate([from_grid, from_mesh], axis=0)
        message = silu(mm_t(link_pick[...], both)).astype(BF)
        table[...] = (mesh_ref[...].astype(F32) + mm(link_pick[grids:, :], message)).astype(BF)

    def ring():
        for d in range(4):
            halo[d] = mm_t(hot(nodes, lists_ref[0, d:d + 1, :]), table[...]).astype(BF)
        for d in range(4):
            border(d).start()

    def project():
        proj[:nodes, :] = mm(table[...], g1[width:2 * width, :]).astype(BF)
        proj[slots:, :] = mm(table[...], g1[2 * width:, :]).astype(BF)
        lists = halo.at[pl.ds(0, 4)]
        pltpu.make_async_copy(lists, lists, hr).wait()
        outer = jnp.concatenate([halo[4 + d] for d in range(4)], axis=0)
        proj[nodes:slots, :] = mm(outer, g1[width:2 * width, :]).astype(BF)

    def hide(part):
        def step(i, carry):
            cols = pl.ds(pl.multiple_of(i * CHUNK, CHUNK), CHUNK)
            before = mm(edges[cols, :], g1[:width, :]) + mm(picks[cols, :], proj[...])
            hidden = silu(before).astype(BF)
            hiddens[cols, :] = hidden
            into[...] += mm(back[:, cols], hidden)
            return carry

        lax.fori_loop(part * chunks // 2, (part + 1) * chunks // 2, step, 0)

    def gather():
        high = into[...].astype(BF)
        low = (into[...] - high.astype(F32)).astype(BF)
        total[...] += mm(high, g2[...]) + mm(low, g2[...])

    steps = {
        "first": begin, "second": rest, "arrive": arrive,
        "turn": functools.partial(take, turns), "direct": functools.partial(take, direct),
        "last": functools.partial(take, last), "lift1": functools.partial(lift, turns),
        "lift2": functools.partial(lift, direct), "lift3": functools.partial(lift, last),
    }
    works = {"mark": mark, "collect": collect, "links": links, "embed": embed, "encode": encode, "ring": ring,
             "project": project, "hide0": functools.partial(hide, 0), "hide1": functools.partial(hide, 1),
             "gather": gather}
    for name, w in PLAN:
        if w is None:
            works[name]()
        else:
            steps[name](w)

    arrive(4)
    incoming = total[...].astype(BF)
    hidden = silu(mm(table[...], h1[:width, :]) + mm(incoming, h1[width:, :])).astype(BF)
    arrive(5)
    latest = (table[...].astype(F32) + mm(hidden, h2[...])).astype(BF)
    lat_out[...] = latest
    weight = jnp.concatenate([area_col[...]] * (width // LANES), axis=1)
    me = face * n_sub + sub
    parts[me] = jnp.sum(latest.astype(F32) * weight, axis=0, keepdims=True)

    def share(k):
        return pltpu.make_async_remote_copy(
            src_ref=parts.at[me], dst_ref=parts.at[me], send_sem=ms, recv_sem=mr,
            device_id=others[k], device_id_type=MESH)

    for k in range(len(others)):
        share(k).start()

    def update(i, carry):
        cols = pl.ds(pl.multiple_of(i * CHUNK, CHUNK), CHUNK)
        edges[cols, :] = (edges[cols, :].astype(F32) + mm(hiddens[cols, :], g2[...])).astype(BF)
        return carry

    lax.fori_loop(0, chunks, update, 0)
    heard = parts.at[pl.ds(0, len(others))]
    pltpu.make_async_copy(heard, heard, mr).wait()
    mass_out[...] = jnp.sum(parts[...], axis=0) / (nodes * n_face * n_sub)

    for w in range(6):
        settle(w, 2 * (n_sub - 1) * cut(w), s1.at[w])
        settle(w, (n_sub - 1) * shards[w].shape[0] // 2, s2.at[w])
        if w in LEVELLED:
            settle(w, 2 * (n_sub - 1) * cut(w), s3.at[LEVELLED.index(w)])
    pltpu.make_async_copy(halo.at[pl.ds(0, 4)], halo.at[pl.ds(0, 4)], hs).wait()
    pltpu.make_async_copy(heard, heard, ms).wait()


def put(lat, edges, mass, lat_out, edges_out, mass_out, sems):
    pairs = [(edges, edges_out), (lat, lat_out), (mass, mass_out)]
    copies = [pltpu.make_async_copy(a, b, sems.at[i]) for i, (a, b) in enumerate(pairs)]
    for copy in copies:
        copy.start()
    for copy in copies:
        copy.wait()


def per_device(
    mesh_latent, edge_latent, grid_features, senders, receivers, send_lists, link_sources,
    link_targets, node_area, grid_weight, encode_weight, edge_first, edge_second, node_first,
    node_second,
):
    n_face, n_sub = lax.axis_size("face"), lax.axis_size("sub")
    nodes, width = mesh_latent.shape
    count = edge_latent.shape[0]
    size = send_lists.shape[2]
    slots = nodes + 4 * size
    chunks = count // CHUNK
    dma = pltpu.SemaphoreType.DMA
    turns = n_sub.bit_length()
    vmem = pl.BlockSpec(memory_space=pltpu.VMEM)
    hbm = pl.BlockSpec(memory_space=pltpu.HBM)
    anywhere = pl.BlockSpec(memory_space=pl.ANY)
    whole = [pltpu.VMEM((n_sub * w.shape[-2], width), BF)
             for w in (encode_weight, edge_first, edge_second, node_first, node_second)]
    results = pl.pallas_call(
        functools.partial(kernel, n_face, n_sub),
        out_shape=(
            pltpu.VMEM(mesh_latent.shape, BF),
            pltpu.VMEM(edge_latent.shape, BF),
            pltpu.VMEM((1, width), F32),
        ),
        in_specs=[hbm] * 15,
        out_specs=(vmem, vmem, vmem),
        scratch_shapes=[
            pltpu.VMEM((n_sub * grid_weight.shape[0], grid_weight.shape[1]), BF), *whole,
            pltpu.VMEM(mesh_latent.shape, BF), pltpu.VMEM(grid_features.shape, BF),
            pltpu.VMEM((1, count), jnp.int32), pltpu.VMEM((1, count), jnp.int32),
            pltpu.VMEM(send_lists.shape, jnp.int32),
            pltpu.VMEM((1, link_sources.shape[0]), jnp.int32),
            pltpu.VMEM((1, link_targets.shape[0]), jnp.int32),
            pltpu.VMEM((1, nodes), F32),
            pltpu.VMEM((count, slots + nodes), BF),
            pltpu.VMEM((nodes, count), BF),
            pltpu.VMEM((grid_features.shape[0] + nodes, link_sources.shape[0]), BF),
            pltpu.VMEM((nodes, width), BF),
            pltpu.VMEM((slots + nodes, width), BF),
            pltpu.VMEM((8, size, width), BF),
            pltpu.VMEM((n_face * n_sub, 1, width), F32),
            pltpu.VMEM((nodes, width), F32),
            pltpu.VMEM((nodes, width), F32),
            pltpu.VMEM(edge_latent.shape, BF),
            pltpu.VMEM((nodes, LANES), F32),
            dma((6,)), dma((6, turns)), dma((6,)), dma((6,)), dma((len(LEVELLED),)), dma((len(LEVELLED), turns)),
            *[dma(())] * 5, dma((6,)), dma((8,)),
        ],
        compiler_params=pltpu.CompilerParams(
            collective_id=0, has_side_effects=True, vmem_limit_bytes=62000000
        ),
    )(
        mesh_latent, edge_latent, grid_features, senders.reshape(1, -1), receivers.reshape(1, -1),
        send_lists, link_sources.reshape(1, -1), link_targets.reshape(1, -1),
        node_area.reshape(1, -1), grid_weight, encode_weight, edge_first, edge_second, node_first,
        node_second,
    )
    return pl.pallas_call(
        put,
        out_shape=tuple(jax.ShapeDtypeStruct(r.shape, r.dtype) for r in results),
        in_specs=[anywhere] * 3,
        out_specs=(anywhere,) * 3,
        scratch_shapes=[dma((3,))],
        compiler_params=pltpu.CompilerParams(vmem_limit_bytes=1 << 20),
    )(*results)


def solution(mesh):
    both = P(("face", "sub"))
    in_specs = (both,) * 9 + (P(None, "sub"), P("sub", None)) + (P(None, "sub", None),) * 4
    return jax.shard_map(
        per_device, mesh=mesh, in_specs=in_specs, out_specs=(both, both, P()), check_vma=False
    )
```

time: 44.4 us -> 38.5 us (0.87)
  Pallas kernels: 43.7 us -> 37.7 us
    pallas_call x1, Pallas kernels: 42.2 us -> 36.3 us  [per_device(): pl.pallas_call(functools.partial(kernel, n_face, n_sub), out_shape=(pltpu...]
where the time goes in v2:
time: 38.5 us; the launch traced here: 38.4 us
  Pallas kernels  37.7 us (98%)
  between operations  0.64 us (2%)
    pallas_call x1, Pallas kernels, per_device(): pl.pallas_call(functools.partial(kernel, n_face, n_sub), out_shape=(pltpu...  36.3 us
    pallas_call x1, Pallas kernels, per_device(): pl.pallas_call(put, out_shape=tuple((jax.ShapeDtypeStruct(r.shape, r.dtyp...  1.42 us

profile of v2, /device:TPU:0, one launch (start us, length us, event | category | flops | bytes accessed | tf_op | source)
XLA Modules:
  0.0 38.4 jit_solution(17994457117893797689)
XLA Ops:
  0.6 36.3 %shard_map.166 = (bf16[256,512]{1,0:T(8,128)(2,1)S(1)}, bf16[2048,512]{1,0:T(8,128)(2,1)S(1)}, f32[1,512]{1,0:T(1,128)S(1)}) custom-call(bf16[256,512]{1,0:T(8,128)(2,1)} %mesh_hbm.1, bf16[2048,512]{1,0:T(8,128)(2,1)} %edge_hbm.1, bf16[256,384]{1,0:T(8,128)(2,1)} %grid_hbm.1, s32[1,2048]{1,0:T(1,128)} %bitcast.5, s32[1,2048]{1,0:T(1,128)} %bitcast.6, ...), custom_call_target="tpu_custom_call" | custom-call | tf_op jit(solution)/shard_map/pallas_call | solution.py:345
  37.0 1.4 %shard_map.167 = (bf16[256,512]{1,0:T(8,128)(2,1)}, bf16[2048,512]{1,0:T(8,128)(2,1)}, f32[1,512]{1,0:T(1,128)}) custom-call(bf16[256,512]{1,0:T(8,128)(2,1)S(1)} %get-tuple-element.6.lat, bf16[2048,512]{1,0:T(8,128)(2,1)S(1)} %get-tuple-element.7.edges, f32[1,512]{1,0:T(1,128)S(1)} %get-tuple-element.8.mass), custom_call_target="tpu_custom_call" | custom-call | tf_op jit(solution)/shard_map/pallas_call | solution.py:385

commit v3 on v2

--- a/solution.py
+++ b/solution.py
@@ -8,7 +8,7 @@
 from jax.sharding import PartitionSpec as P
 
 MESH = pl.DeviceIdType.MESH
-CHUNK = 512
+CHUNK = 1024
 LANES = 128
 LEVELLED = (1, 4)
 BF = jnp.bfloat16
@@ -33,14 +33,15 @@
 
 
 PLAN = (
-    ("first", 1), ("first", 0), ("second", 0), ("second", 1), ("first", 4), ("turn", 1), ("turn", 0),
-    ("first", 2), ("direct", 1), ("last", 1), ("turn", 4), ("last", 0), ("second", 2), ("links", None),
-    ("direct", 0), ("lift1", 1), ("mark", None), ("turn", 2), ("collect", None), ("lift2", 1), ("first", 5),
-    ("lift3", 1), ("second", 4), ("first", 3), ("last", 4), ("arrive", 0), ("embed", None), ("second", 3),
-    ("lift1", 4), ("arrive", 1), ("encode", None), ("ring", None), ("second", 5), ("direct", 2), ("last", 2),
-    ("direct", 4), ("turn", 5), ("arrive", 2), ("turn", 3), ("project", None), ("direct", 3), ("hide0", None),
-    ("direct", 5), ("lift2", 4), ("last", 5), ("last", 3), ("lift3", 4), ("hide1", None), ("arrive", 3),
-    ("gather", None),
+    ("first", 1), ("first", 4), ("mark", None), ("first", 0), ("second", 1), ("collect", None), ("second", 4),
+    ("turn", 1), ("second", 0), ("first", 2), ("turn", 0), ("direct", 1), ("last", 1), ("direct", 0),
+    ("second", 2), ("lift1", 1), ("links", None), ("turn", 2), ("last", 0), ("lift2", 1), ("lift3", 1),
+    ("first", 3), ("arrive", 0), ("turn", 4), ("embed", None), ("direct", 2), ("arrive", 1), ("first", 5),
+    ("second", 3), ("encode", None), ("ring", None), ("last", 2), ("turn", 3), ("direct", 4), ("arrive", 2),
+    ("lift1", 4), ("last", 4), ("project", None), ("turn", 5), ("second", 5), ("near0", None),
+    ("near1", None), ("direct", 3), ("last", 3), ("lift2", 4), ("outer", None), ("far1", None), ("lift3", 4),
+    ("direct", 5), ("last", 5), ("far0", None), ("arrive", 3), ("gather", None), ("arrive", 4),
+    ("node", None),
 )
 
 
@@ -51,7 +52,7 @@
     lat_out, edges, mass_out,
     gg, ge, g1, g2, h1, h2,
     mesh_ref, grid_ref, send_ref, recv_ref, lists_ref, src_ref, dst_ref, area_ref,
-    picks, back, link_pick, table, proj, halo, parts, total, into, hiddens, area_col,
+    picks, back, link_pick, table, proj, halo, parts, total, into, ahead, partial, hiddens, area_col,
     s1, r1, s2, r2, s3, r3, hs, hr, ms, mr, ein, win, pin,
 ):
     face, sub = lax.axis_index("face"), lax.axis_index("sub")
@@ -79,10 +80,12 @@
     pairs = [(send_hbm, send_ref), (recv_hbm, recv_ref), (src_hbm, src_ref), (dst_hbm, dst_ref),
              (grid_hbm, grid_ref), (mesh_hbm, mesh_ref), (lists_hbm, lists_ref), (area_hbm, area_ref)]
     loads = [pltpu.make_async_copy(a, b, pin.at[i]) for i, (a, b) in enumerate(pairs)]
-    for w in range(6):
+    for w in (1, 0, 4):
         own(w).start()
     for copy in loads:
         copy.start()
+    for w in (2, 3, 5):
+        own(w).start()
     load_edges.start()
 
     others = [(lax.rem(face + a, n_face), lax.rem(sub + b, n_sub))
@@ -202,8 +205,9 @@
             cols = pl.ds(pl.multiple_of(i * CHUNK, CHUNK), CHUNK)
             here = hot(nodes, recv_ref[:, cols])
             back[:, cols] = here
-            both = jnp.concatenate([hot(slots, send_ref[:, cols]), here], axis=0)
-            picks[cols, :] = both.T
+            from_own = hot(nodes, send_ref[:, cols])
+            from_other = hot(slots - nodes, send_ref[:, cols] - nodes)
+            picks[cols, :] = jnp.concatenate([from_own, here, from_other], axis=0).T
             return carry
 
         lax.fori_loop(0, chunks, step, 0)
@@ -241,22 +245,27 @@
 
     def project():
         proj[:nodes, :] = mm(table[...], g1[width:2 * width, :]).astype(BF)
-        proj[slots:, :] = mm(table[...], g1[2 * width:, :]).astype(BF)
+        proj[nodes:2 * nodes, :] = mm(table[...], g1[2 * width:, :]).astype(BF)
+
+    def outer():
         lists = halo.at[pl.ds(0, 4)]
         pltpu.make_async_copy(lists, lists, hr).wait()
-        outer = jnp.concatenate([halo[4 + d] for d in range(4)], axis=0)
-        proj[nodes:slots, :] = mm(outer, g1[width:2 * width, :]).astype(BF)
-
-    def hide(part):
-        def step(i, carry):
-            cols = pl.ds(pl.multiple_of(i * CHUNK, CHUNK), CHUNK)
-            before = mm(edges[cols, :], g1[:width, :]) + mm(picks[cols, :], proj[...])
-            hidden = silu(before).astype(BF)
-            hiddens[cols, :] = hidden
-            into[...] += mm(back[:, cols], hidden)
-            return carry
-
-        lax.fori_loop(part * chunks // 2, (part + 1) * chunks // 2, step, 0)
+        rows = jnp.concatenate([halo[4 + d] for d in range(4)], axis=0)
+        proj[2 * nodes:, :] = mm(rows, g1[width:2 * width, :]).astype(BF)
+
+    def near(i):
+        rows = slice(i * CHUNK, (i + 1) * CHUNK)
+        partial[rows, :] = mm(edges[rows, :], g1[:width, :]) + mm(picks[rows, :2 * nodes], proj[:2 * nodes, :])
+
+    def far(i):
+        rows = slice(i * CHUNK, (i + 1) * CHUNK)
+        before = partial[rows, :] + mm(picks[rows, 2 * nodes:], proj[2 * nodes:, :])
+        hidden = silu(before).astype(BF)
+        hiddens[rows, :] = hidden
+        into[...] += mm(back[:, rows], hidden)
+
+    def begin_node():
+        ahead[...] = mm(table[...], h1[:width, :])
 
     def gather():
         high = into[...].astype(BF)
@@ -270,17 +279,18 @@
         "lift2": functools.partial(lift, direct), "lift3": functools.partial(lift, last),
     }
     works = {"mark": mark, "collect": collect, "links": links, "embed": embed, "encode": encode, "ring": ring,
-             "project": project, "hide0": functools.partial(hide, 0), "hide1": functools.partial(hide, 1),
-             "gather": gather}
+             "project": project, "outer": outer, "gather": gather, "node": begin_node}
+    for i in range(chunks):
+        works[f"near{i}"] = functools.partial(near, i)
+        works[f"far{i}"] = functools.partial(far, i)
     for name, w in PLAN:
         if w is None:
             works[name]()
         else:
             steps[name](w)
 
-    arrive(4)
     incoming = total[...].astype(BF)
-    hidden = silu(mm(table[...], h1[:width, :]) + mm(incoming, h1[width:, :])).astype(BF)
+    hidden = silu(ahead[...] + mm(incoming, h1[width:, :])).astype(BF)
     arrive(5)
     latest = (table[...].astype(F32) + mm(hidden, h2[...])).astype(BF)
     lat_out[...] = latest
@@ -368,6 +378,8 @@
             pltpu.VMEM((n_face * n_sub, 1, width), F32),
             pltpu.VMEM((nodes, width), F32),
             pltpu.VMEM((nodes, width), F32),
+            pltpu.VMEM((nodes, width), F32),
+            pltpu.VMEM(edge_latent.shape, F32),
             pltpu.VMEM(edge_latent.shape, BF),
             pltpu.VMEM((nodes, LANES), F32),
             dma((6,)), dma((6, turns)), dma((6,)), dma((6,)), dma((len(LEVELLED),)), dma((len(LEVELLED), turns)),

time: 38.5 us -> 35.7 us (0.927)
  Pallas kernels: 37.7 us -> 35 us
    pallas_call x1, Pallas kernels: 36.3 us -> 33.5 us  [per_device(): pl.pallas_call(functools.partial(kernel, n_face, n_sub), out_shape=(pltpu...]
where the time goes in v3:
time: 35.7 us; the launch traced here: 35.6 us
  Pallas kernels  35 us (98%)
  between operations  0.64 us (2%)
    pallas_call x1, Pallas kernels, per_device(): pl.pallas_call(functools.partial(kernel, n_face, n_sub), out_shape=(pltpu...  33.5 us
    pallas_call x1, Pallas kernels, per_device(): pl.pallas_call(put, out_shape=tuple((jax.ShapeDtypeStruct(r.shape, r.dtyp...  1.42 us

profile of v3, /device:TPU:0, one launch (start us, length us, event | category | flops | bytes accessed | tf_op | source)
XLA Modules:
  0.0 35.6 jit_solution(15247885073451710906)
XLA Ops:
  0.6 33.5 %shard_map.166 = (bf16[256,512]{1,0:T(8,128)(2,1)S(1)}, bf16[2048,512]{1,0:T(8,128)(2,1)S(1)}, f32[1,512]{1,0:T(1,128)S(1)}) custom-call(bf16[256,512]{1,0:T(8,128)(2,1)} %mesh_hbm.1, bf16[2048,512]{1,0:T(8,128)(2,1)} %edge_hbm.1, bf16[256,384]{1,0:T(8,128)(2,1)} %grid_hbm.1, s32[1,2048]{1,0:T(1,128)} %bitcast.5, s32[1,2048]{1,0:T(1,128)} %bitcast.6, ...), custom_call_target="tpu_custom_call" | custom-call | tf_op jit(solution)/shard_map/pallas_call | solution.py:355
  34.2 1.4 %shard_map.167 = (bf16[256,512]{1,0:T(8,128)(2,1)}, bf16[2048,512]{1,0:T(8,128)(2,1)}, f32[1,512]{1,0:T(1,128)}) custom-call(bf16[256,512]{1,0:T(8,128)(2,1)S(1)} %get-tuple-element.6.lat, bf16[2048,512]{1,0:T(8,128)(2,1)S(1)} %get-tuple-element.7.edges, f32[1,512]{1,0:T(1,128)S(1)} %get-tuple-element.8.mass), custom_call_target="tpu_custom_call" | custom-call | tf_op jit(solution)/shard_map/pallas_call | solution.py:397
